TPU v7x, 256 devices: a whole 4x4x8 slice. The times are simulated.
256 devices in a mesh: section: 8 (over z), ex: 4 (over x), ey: 8 (over y, core).
Axes of the slice: x: 4, y: 4, z: 8, core: 2. Of those that a mesh axis runs over, the one named last changes fastest.
Arguments:
- section_out: bfloat16 [8, 2048, 7168], P('section', ('ex', 'ey')), may hold values from -6 to 6
- expert_ids: int32 [8, 2048, 2], P('section', ('ex', 'ey')), may hold values from 0 to 7, all different within a row; in each aligned block of 64 rows (0 to 63, 64 to 127, ..., all dimensions but the last counted through in order) at most 24 rows name the same one
- gate_weights: float32 [8, 2048, 2], P('section', ('ex', 'ey')), may hold values from 0.1 to 1
- w_gate_up: bfloat16 [8, 8, 7168, 2, 1024], P('section', 'ey', None, None, 'ex'), may hold values from -0.0625 to 0.0625
- w_down: bfloat16 [8, 8, 1024, 7168], P('section', 'ey', 'ex'), may hold values from -0.1875 to 0.1875
Outputs:
- next_state: bfloat16 [8, 2048, 7168], P('section', ('ex', 'ey'))
Inputs may be any that keep to these rules, and one draw needn't show every extreme that they name: `expert_ids`: each row names 2 different experts. In the rows of one device (aligned blocks of 64 rows, all leading dimensions in order) no expert is named by more than 24 rows, and some block of every draw names one expert exactly 24 times.
All inputs are finite; a program needn't handle non-finite values.
Results may differ from a plain program's by a relative error of at most 0.008.
Values may be sent and summed in bfloat16 or wider, within the bound.
A program may use at most 128 MiB of HBM per device.

v0:
```python
import jax
import jax.numpy as jnp
from jax import lax
from jax.sharding import PartitionSpec as P


def shifted(value, axis, steps):
    count = lax.axis_size(axis)
    pairs = [(source, (source + steps) % count) for source in range(count)]
    return lax.ppermute(value, axis, pairs)


def expert_hidden(token_rows, gate_up, unit_count):
    mixed = jnp.dot(token_rows, gate_up, preferred_element_type=jnp.float32)
    return (jax.nn.silu(mixed[:, :unit_count]) * mixed[:, unit_count:]).astype(jnp.bfloat16)


def on_device(section_out, expert_ids, gate_weights, w_gate_up, w_down):
    tok_rows = section_out.shape[1]
    model_width = section_out.shape[2]
    top_count = expert_ids.shape[2]
    experts = lax.axis_size("ey")
    capacity = min(tok_rows, 3 * tok_rows * top_count // (2 * experts))
    unit_count = w_down.shape[2]
    gate_up = w_gate_up[0, 0].reshape(model_width, 2 * unit_count)
    down_rows = w_down[0, 0]
    incoming = shifted(section_out, "section", 1)[0]
    chosen = expert_ids[0].reshape(-1)
    one_hot = (chosen[:, None] == jnp.arange(experts, dtype=jnp.int32)[None, :]).astype(jnp.int32)
    slot_rank = jnp.sum((jnp.cumsum(one_hot, axis=0) - one_hot) * one_hot, axis=1)
    position = chosen * capacity + slot_rank
    token_of = jnp.arange(tok_rows * top_count, dtype=jnp.int32) // top_count
    filled = jnp.zeros((experts * capacity,), jnp.int32).at[position].set(1)
    source_row = jnp.zeros((experts * capacity,), jnp.int32).at[position].set(token_of)
    outgoing = jnp.where(filled[:, None] > 0, incoming[source_row], jnp.zeros((), jnp.bfloat16))
    arrived = lax.all_to_all(
        outgoing.reshape(experts, capacity, model_width),
        "ey",
        split_axis=0,
        concat_axis=0,
        tiled=True,
    ).reshape(experts * capacity, model_width)
    hidden_all = expert_hidden(
        lax.all_gather(arrived, "ex", axis=0, tiled=True), gate_up, unit_count
    )
    summed = lax.psum_scatter(
        jnp.dot(hidden_all, down_rows, preferred_element_type=jnp.float32).astype(jnp.bfloat16),
        "ex",
        scatter_dimension=0,
        tiled=True,
    )
    expert_out = lax.all_to_all(
        summed.reshape(experts, capacity, model_width),
        "ey",
        split_axis=0,
        concat_axis=0,
        tiled=True,
    ).reshape(experts * capacity, model_width)
    picked = expert_out[position].reshape(tok_rows, top_count, model_width)
    weighted = jnp.einsum("tkd,tk->td", picked.astype(jnp.float32), gate_weights[0])
    result = (incoming.astype(jnp.float32) + weighted).astype(jnp.bfloat16)
    return result[None]


def solution(mesh):
    return jax.shard_map(
        on_device,
        mesh=mesh,
        in_specs=(
            P("section", ("ex", "ey"), None),
            P("section", ("ex", "ey"), None),
            P("section", ("ex", "ey"), None),
            P("section", "ey", None, None, "ex"),
            P("section", "ey", "ex", None),
        ),
        out_specs=P("section", ("ex", "ey"), None),
        check_vma=False,
    )
```

profile of v0, /device:TPU:1, one launch (start us, length us, event | category | flops | bytes accessed | tf_op | source)
XLA Modules:
  0.0 363.6 jit_solution(1292893236069667634)
XLA Ops:
  6.5 2.5 collective-permute-start
  9.0 0.8 copy.9
  9.8 0.7 broadcast_multiply_fusion
  10.4 0.1 eq.15
  10.6 0.1 fusion.6
  10.7 0.1 copy.8
  10.8 0.1 mul.28
  10.9 0.2 reduce_window_sum.11
  11.1 0.2 select_reduce_fusion
  11.3 1.0 scatter_custom_fusion.1
  12.3 1.0 scatter_custom_fusion
  13.3 0.1 broadcast_in_dim.29
  13.4 19.8 %collective-permute-done = bf16[1,64,7168]{2,1,0:T(8,128)(2,1)S(1)} collective-permute-done((bf16[1,64,7168]{2,1,0:T(8,128)(2,1)}, bf16[1,64,7168]{2,1,0:T(8,128)(2,1)S(1)}, u32[]{:S(2)}, u32[]{:S(2)}) %collective-permute-start) | collective-permute-done | bytes 917536 | tf_op jit(solution)/shard_map/ppermute | solution.py:10
  33.2 3.8 %gather_fusion = bf16[192,7168]{1,0:T(8,128)(2,1)} fusion(bf16[64,7168]{1,0:T(8,128)(2,1)S(1)} %bitcast.32, s32[1024]{0:T(1024)S(1)} %pad_clamp_fusion.1), kind=kCustom, calls=%fused_computation | custom fusion | bytes 5505792 | tf_op jit(solution)/shard_map/gather | solution.py:35
  37.0 2.0 broadcast_select_fusion
  39.1 39.0 %all_to_all.10 = bf16[8,24,7168]{2,1,0:T(8,128)(2,1)} all-to-all(bf16[8,24,7168]{2,1,0:T(8,128)(2,1)S(1)} %broadcast_select_fusion), channel_id=1, replica_groups=mesh['section'=8,'ex'=4,'ey'=8] {'ey'}, dimensions={0} | all-to-all | bytes 5505024 | tf_op jit(solution)/shard_map/all_to_all | solution.py:36
  78.1 0.0 all-gather.2.cloned.1.call-update
  78.1 0.0 reduce-scatter.2.cloned.1.call-start
  78.1 7.4 %copy.12 = bf16[896,8,2,256]{3,1,2,0:T(8,128)(2,1)} copy(bf16[896,8,2,256]{3,2,1,0:T(2,128)(2,1)} %bitcast.35) | data formatting | bytes 14680064
  85.5 98.6 %all-gather.2.cloned.1.call-done = bf16[768,7168]{1,0:T(8,128)(2,1)} async-done(((bf16[192,7168]{1,0:T(8,128)(2,1)}), bf16[768,7168]{1,0:T(8,128)(2,1)}) %all-gather.2.cloned.1.call-update) | async-done | bytes 11010064 | tf_op jit(solution)/shard_map/all_gather | solution.py:44
  184.1 10.9 %fusion.13 = f32[768,512]{1,0:T(8,128)S(1)} fusion(bf16[768,7168]{1,0:T(8,128)(2,1)} %all-gather.2.cloned.1.call-done, bf16[7168,512]{1,0:T(8,128)(2,1)} %bitcast.36), kind=kOutput, calls=%fused_computation.33 | convolution fusion | flops 5637144576 | bytes 19922944 | tf_op jit(solution)/shard_map/dot_general | solution.py:14
  195.0 5.8 %convolution_convert_fusion = bf16[768,7168]{1,0:T(8,128)(2,1)} fusion(bf16[1,1,256,7168]{3,2,1,0:T(8,128)(2,1)S(1)} %copy-done, f32[768,512]{1,0:T(8,128)S(1)} %fusion.13), kind=kOutput, calls=%fused_computation.4 | convolution fusion | flops 2825256960 | bytes 16252928 | tf_op jit(solution)/shard_map/dot_general | solution.py:47
  200.7 0.0 reduce-scatter.2.cloned.1.call-update
  200.8 105.6 %reduce-scatter.2.cloned.1.call-done = bf16[192,7168]{1,0:T(8,128)(2,1)} async-done(((bf16[768,7168]{1,0:T(8,128)(2,1)}), bf16[192,7168]{1,0:T(8,128)(2,1)}) %reduce-scatter.2.cloned.1.call-update) | async-done | bytes 2752528 | tf_op jit(solution)/shard_map/reduce_scatter | solution.py:46
  306.3 5.1 %all-to-all-start.1 = ((bf16[8,24,7168]{2,1,0:T(8,128)(2,1)}), bf16[8,24,7168]{2,1,0:T(8,128)(2,1)}, u32[]{:S(2)}, u32[]{:S(2)}) async-start(bf16[8,24,7168]{2,1,0:T(8,128)(2,1)} %bitcast.37), calls=%async_computation.2 | async-start | bytes 5505024 | tf_op jit(solution)/shard_map/all_to_all | solution.py:52
  311.5 0.0 copy-done.1
  311.5 0.1 copy.10
  311.6 33.2 %all-to-all-done.1 = bf16[8,24,7168]{2,1,0:T(8,128)(2,1)} async-done(((bf16[8,24,7168]{2,1,0:T(8,128)(2,1)}), bf16[8,24,7168]{2,1,0:T(8,128)(2,1)}, u32[]{:S(2)}, u32[]{:S(2)}) %all-to-all-start.1) | async-done | bytes 2752544 | tf_op jit(solution)/shard_map/all_to_all | solution.py:52
  344.8 5.5 %gather_fusion.1 = bf16[128,7168]{1,0:T(8,128)(2,1)S(1)} fusion(bf16[192,7168]{1,0:T(8,128)(2,1)} %bitcast.7, s32[1024]{0:T(1024)S(1)} %pad_clamp_fusion), kind=kCustom, calls=%fused_computation.1 | custom fusion | bytes 3670528 | tf_op jit(solution)/shard_map/gather | solution.py:59
  350.3 1.7 reshape.53
  352.0 3.5 fusion.14
  355.5 1.3 fusion.2
  (11 shorter events, 0.0 us)
Async XLA Ops:
  6.5 177.5 %all-gather.2.cloned.1.call-start = ((), (), s32[]{:S(2)}) async-start(), calls=%async_computation.3 | async-start | bytes 13762560 | tf_op jit(solution)/shard_map/all_gather | solution.py:44
  6.5 26.7 %collective-permute-start = (bf16[1,64,7168]{2,1,0:T(8,128)(2,1)}, bf16[1,64,7168]{2,1,0:T(8,128)(2,1)S(1)}, u32[]{:S(2)}, u32[]{:S(2)}) collective-permute-start(bf16[1,64,7168]{2,1,0:T(8,128)(2,1)} %param.5), channel_id=1, source_target_pairs={{0,32},{32,64},{64,96},{96,128},{128,160},{160,192},{192,224},{224... | collective-permute-start | bytes 2752520 | tf_op jit(solution)/shard_map/ppermute | solution.py:10
  78.1 228.2 %reduce-scatter.2.cloned.1.call-start = ((), (), s32[]{:S(2)}) async-start(), calls=%async_computation.4 | async-start | bytes 13762560 | tf_op jit(solution)/shard_map/reduce_scatter | solution.py:46
  184.1 10.9 %copy-start = (bf16[1,1,256,7168]{3,2,1,0:T(8,128)(2,1)S(1)}, bf16[1,1,256,7168]{3,2,1,0:T(8,128)(2,1)}, u32[]{:S(2)}) copy-start(bf16[1,1,256,7168]{3,2,1,0:T(8,128)(2,1)} %param.9) | copy-start | bytes 11010052
  306.3 5.2 %copy-start.1 = (f32[1,64,2]{1,2,0:T(2,128)S(1)}, f32[1,64,2]{1,2,0:T(2,128)}, u32[]{:S(2)}) copy-start(f32[1,64,2]{1,2,0:T(2,128)} %param.7) | copy-start | bytes 1540
  306.3 38.5 %all-to-all-start.1 = ((bf16[8,24,7168]{2,1,0:T(8,128)(2,1)}), bf16[8,24,7168]{2,1,0:T(8,128)(2,1)}, u32[]{:S(2)}, u32[]{:S(2)}) async-start(bf16[8,24,7168]{2,1,0:T(8,128)(2,1)} %bitcast.37), calls=%async_computation.2 | async-start | bytes 5505024 | tf_op jit(solution)/shard_map/all_to_all | solution.py:52
Sparse Core Ops, SparseCore 0:
  78.2 105.8 all-gather.1
  200.9 105.3 reduce-scatter.1
where the time goes:
time: 364 us
  waiting for transfers between devices  257 us (71%)
  blocking collectives  39 us (11%)
  local copies, waits for them, and re-layouts  21.7 us (6%)
  matrix products  20.2 us (6%)
  between operations  13.5 us (4%)
  starting transfers between devices  7.65 us (2%)
  other arithmetic  4.43 us (1%)
    reduce_scatter x1, waiting for transfers between devices, on_device(): lax.psum_scatter(jnp.dot(hidden_all, down_rows, preferred_element_type=jn...  106 us
    all_gather x1, waiting for transfers between devices, on_device(): lax.all_gather(arrived, 'ex', axis=0, tiled=True)  98.6 us
    all_to_all x1, blocking collectives, on_device(): lax.all_to_all(outgoing.reshape(experts, capacity, model_width), 'ey', sp...  39 us
    all_to_all x1, waiting for transfers between devices, on_device(): lax.all_to_all(summed.reshape(experts, capacity, model_width), 'ey', spli...  33.2 us
    ppermute x1, waiting for transfers between devices, shifted(): return lax.ppermute(value, axis, pairs)  19.8 us
    dot_general x1, matrix products, expert_hidden(): mixed = jnp.dot(token_rows, gate_up, preferred_element_type=jnp.float32)  10.9 us
    unnamed x6, local copies, waits for them, and re-layouts  8.14 us
  transfers between devices with their start and end apart: 4, of which 4 were waited for; matrix products, arithmetic and copies ran while one was open for 3% of the time, Pallas kernels for 0%

commit v1 on v0

--- a/solution.py
+++ b/solution.py
@@ -40,9 +40,32 @@
         concat_axis=0,
         tiled=True,
     ).reshape(experts * capacity, model_width)
-    hidden_all = expert_hidden(
-        lax.all_gather(arrived, "ex", axis=0, tiled=True), gate_up, unit_count
-    )
+
+    def lead_axis_part(xx):
+        oldest, piece_next, opened = (
+            jax.lax.axis_size("ex"),
+            jax.lax.axis_index("ex"),
+            xx.shape[0],
+        )
+        table = [(idx, (idx + 1) % oldest) for idx in range(oldest)]
+        block_list = [(idx, (idx - 1) % oldest) for idx in range(oldest)]
+        k_now = jnp.zeros((*xx.shape[:0], oldest * opened, *xx.shape[1:]), xx.dtype)
+        k_now = lax.dynamic_update_slice_in_dim(k_now, xx, piece_next * opened, axis=0)
+        kept_arr = local_next = xx
+        moved = oldest // 2
+        for dev_i in tuple(range(1, moved + 1)):
+            kept_arr = jax.lax.ppermute(kept_arr, "ex", table)
+            k_now = lax.dynamic_update_slice_in_dim(
+                k_now, kept_arr, (piece_next - dev_i) % oldest * opened, axis=0
+            )
+            if dev_i < oldest - moved:
+                local_next = jax.lax.ppermute(local_next, "ex", block_list)
+                k_now = lax.dynamic_update_slice_in_dim(
+                    k_now, local_next, (piece_next + dev_i) % oldest * opened, axis=0
+                )
+        return k_now
+
+    hidden_all = expert_hidden(lead_axis_part(arrived), gate_up, unit_count)
     summed = lax.psum_scatter(
         jnp.dot(hidden_all, down_rows, preferred_element_type=jnp.float32).astype(jnp.bfloat16),
         "ex",

time: 364 us -> 377 us (1.036)
  local copies, waits for them, and re-layouts: 21.7 us -> 31.7 us
    ppermute x0 -> x3, waiting for transfers between devices: none -> 105 us  [the longest x2 105 us: lead_axis_part(): kept_arr = jax.lax.ppermute(kept_arr, 'ex', table)]
    all_gather x1 -> x0, waiting for transfers between devices: 98.6 us -> none  [on_device(): lax.all_gather(arrived, 'ex', axis=0, tiled=True)]
    dynamic_update_slice x0 -> x4, local copies, waits for them, and re-layouts: none -> 8.73 us  [the longest x2 4.36 us: lead_axis_part(): lax.dynamic_update_slice_in_dim(k_now, kept_arr, (piece_next - dev_i) % o...]
    dot_general x1, matrix products: 10.9 us -> 6.96 us  [expert_hidden(): mixed = jnp.dot(token_rows, gate_up, preferred_element_type=jnp.float32)]
    unnamed x6 -> x10, local copies, waits for them, and re-layouts: 8.14 us -> 8.11 us
  transfers between devices with their start and end apart: 4 -> 6, of which waited for: 4 -> 5; matrix products, arithmetic and copies ran while one was open for 3% -> 5% of each run, Pallas kernels for 0% -> 0%
where the time goes in v1:
time: 377 us
  waiting for transfers between devices  260 us (69%)
  blocking collectives  39 us (10%)
  local copies, waits for them, and re-layouts  31.7 us (8%)
  matrix products  17.7 us (5%)
  between operations  13.6 us (4%)
  starting transfers between devices  10.3 us (3%)
  other arithmetic  4.43 us (1%)
    ppermute x2, waiting for transfers between devices, lead_axis_part(): kept_arr = jax.lax.ppermute(kept_arr, 'ex', table)  105 us
    reduce_scatter x1, waiting for transfers between devices, on_device(): lax.psum_scatter(jnp.dot(hidden_all, down_rows, preferred_element_type=jn...  102 us
    all_to_all x1, blocking collectives, on_device(): lax.all_to_all(outgoing.reshape(experts, capacity, model_width), 'ey', sp...  39 us
    all_to_all x1, waiting for transfers between devices, on_device(): lax.all_to_all(summed.reshape(experts, capacity, model_width), 'ey', spli...  33.2 us
    ppermute x1, waiting for transfers between devices, shifted(): return lax.ppermute(value, axis, pairs)  19.8 us
    unnamed x10, local copies, waits for them, and re-layouts  8.11 us
  transfers between devices with their start and end apart: 6, of which 5 were waited for; matrix products, arithmetic and copies ran while one was open for 5% of the time, Pallas kernels for 0%

profile of v1, /device:TPU:1, one launch (start us, length us, event | category | flops | bytes accessed | tf_op | source)
XLA Modules:
  0.0 376.8 jit_solution(10377472866339742364)
XLA Ops:
  6.5 2.5 collective-permute-start
  9.0 0.8 copy.9
  9.8 0.7 broadcast_multiply_fusion
  10.4 0.1 eq.19
  10.8 0.1 mul.40
  10.9 0.2 reduce_window_sum.11
  11.1 0.2 select_reduce_fusion
  11.3 1.0 scatter_custom_fusion.1
  12.3 1.0 scatter_custom_fusion
  13.4 19.8 %collective-permute-done = bf16[1,64,7168]{2,1,0:T(8,128)(2,1)S(1)} collective-permute-done((bf16[1,64,7168]{2,1,0:T(8,128)(2,1)}, bf16[1,64,7168]{2,1,0:T(8,128)(2,1)S(1)}, u32[]{:S(2)}, u32[]{:S(2)}) %collective-permute-start) | collective-permute-done | bytes 917536 | tf_op jit(solution)/shard_map/ppermute | solution.py:10
  33.2 3.9 %gather_fusion = bf16[192,7168]{1,0:T(8,128)(2,1)} fusion(bf16[64,7168]{1,0:T(8,128)(2,1)S(1)} %bitcast.32, s32[1024]{0:T(1024)S(1)} %pad_clamp_fusion.1), kind=kCustom, calls=%fused_computation | custom fusion | bytes 5505792 | tf_op jit(solution)/shard_map/gather | solution.py:35
  37.0 2.0 broadcast_select_fusion
  39.1 39.0 %all_to_all.10 = bf16[8,24,7168]{2,1,0:T(8,128)(2,1)} all-to-all(bf16[8,24,7168]{2,1,0:T(8,128)(2,1)S(1)} %broadcast_select_fusion), channel_id=1, replica_groups=mesh['section'=8,'ex'=4,'ey'=8] {'ey'}, dimensions={0} | all-to-all | bytes 5505024 | tf_op jit(solution)/shard_map/all_to_all | solution.py:36
  78.1 1.2 collective-permute-start.1
  79.3 1.5 collective-permute-start.2
  80.7 59.2 %collective-permute-done.1 = bf16[192,7168]{1,0:T(8,128)(2,1)} collective-permute-done((bf16[192,7168]{1,0:T(8,128)(2,1)}, bf16[192,7168]{1,0:T(8,128)(2,1)}, u32[]{:S(2)}, u32[]{:S(2)}) %collective-permute-start.1) | collective-permute-done | bytes 2752544 | tf_op jit(solution)/shard_map/ppermute | solution.py:57
  140.0 7.3 %copy.12 = bf16[896,8,2,256]{3,1,2,0:T(8,128)(2,1)} copy(bf16[896,8,2,256]{3,2,1,0:T(2,128)(2,1)} %bitcast.34) | data formatting | bytes 14680064
  147.3 1.3 broadcast_in_dim.31
  148.6 2.1 constant_dynamic-update-slice_fusion.2
  150.8 2.3 constant_dynamic-update-slice_fusion.1
  153.1 2.3 constant_dynamic-update-slice_fusion
  155.3 45.7 %collective-permute-done.3 = bf16[192,7168]{1,0:T(8,128)(2,1)} collective-permute-done((bf16[192,7168]{1,0:T(8,128)(2,1)}, bf16[192,7168]{1,0:T(8,128)(2,1)}, u32[]{:S(2)}, u32[]{:S(2)}) %collective-permute-start.3) | collective-permute-done | bytes 2752544 | tf_op jit(solution)/shard_map/ppermute | solution.py:57
  201.0 2.1 constant_dynamic-update-slice_fusion.3
  203.2 7.0 %fusion.13 = f32[768,512]{1,0:T(8,128)} fusion(bf16[768,7168]{1,0:T(8,128)(2,1)S(1)} %constant_dynamic-update-slice_fusion.3, bf16[7168,512]{1,0:T(8,128)(2,1)S(1)} %bitcast.37), kind=kOutput, calls=%fused_computation.37 | convolution fusion | flops 5637144576 | bytes 19922944 | tf_op jit(solution)/shard_map/dot_general | solution.py:14
  210.1 7.2 %convolution_convert_fusion = bf16[768,7168]{1,0:T(8,128)(2,1)} fusion(bf16[1,1,256,7168]{3,2,1,0:T(8,128)(2,1)S(1)} %copy-done, f32[768,512]{1,0:T(8,128)} %fusion.13), kind=kOutput, calls=%fused_computation.4 | convolution fusion | flops 2825256960 | bytes 16252928 | tf_op jit(solution)/shard_map/dot_general | solution.py:70
  217.4 102.1 %reduce-scatter.2.cloned.1.call-done = bf16[192,7168]{1,0:T(8,128)(2,1)} async-done(((bf16[768,7168]{1,0:T(8,128)(2,1)}), bf16[192,7168]{1,0:T(8,128)(2,1)}) %reduce-scatter.2.cloned.1.call-update) | async-done | bytes 2752528 | tf_op jit(solution)/shard_map/reduce_scatter | solution.py:69
  319.5 5.2 %all-to-all-start.1 = ((bf16[8,24,7168]{2,1,0:T(8,128)(2,1)}), bf16[8,24,7168]{2,1,0:T(8,128)(2,1)}, u32[]{:S(2)}, u32[]{:S(2)}) async-start(bf16[8,24,7168]{2,1,0:T(8,128)(2,1)} %bitcast.38), calls=%async_computation.2 | async-start | bytes 5505024 | tf_op jit(solution)/shard_map/all_to_all | solution.py:75
  324.8 33.2 %all-to-all-done.1 = bf16[8,24,7168]{2,1,0:T(8,128)(2,1)} async-done(((bf16[8,24,7168]{2,1,0:T(8,128)(2,1)}), bf16[8,24,7168]{2,1,0:T(8,128)(2,1)}, u32[]{:S(2)}, u32[]{:S(2)}) %all-to-all-start.1) | async-done | bytes 2752544 | tf_op jit(solution)/shard_map/all_to_all | solution.py:75
  358.0 5.5 %gather_fusion.1 = bf16[128,7168]{1,0:T(8,128)(2,1)S(1)} fusion(bf16[192,7168]{1,0:T(8,128)(2,1)} %bitcast.7, s32[1024]{0:T(1024)S(1)} %pad_clamp_fusion), kind=kCustom, calls=%fused_computation.1 | custom fusion | bytes 3670528 | tf_op jit(solution)/shard_map/gather | solution.py:82
  363.5 1.7 reshape.53
  365.2 3.5 fusion.14
  368.7 1.3 fusion.2
  (24 shorter events, 0.5 us)
Async XLA Ops:
  6.5 312.9 %reduce-scatter.2.cloned.1.call-start = ((), (), s32[]{:S(2)}) async-start(), calls=%async_computation.3 | async-start | bytes 13762560 | tf_op jit(solution)/shard_map/reduce_scatter | solution.py:69
  6.5 26.7 %collective-permute-start = (bf16[1,64,7168]{2,1,0:T(8,128)(2,1)}, bf16[1,64,7168]{2,1,0:T(8,128)(2,1)S(1)}, u32[]{:S(2)}, u32[]{:S(2)}) collective-permute-start(bf16[1,64,7168]{2,1,0:T(8,128)(2,1)} %param.5), channel_id=1, source_target_pairs={{0,32},{32,64},{64,96},{96,128},{128,160},{160,192},{192,224},{224... | collective-permute-start | bytes 2752520 | tf_op jit(solution)/shard_map/ppermute | solution.py:10
  78.1 61.9 %collective-permute-start.1 = (bf16[192,7168]{1,0:T(8,128)(2,1)}, bf16[192,7168]{1,0:T(8,128)(2,1)}, u32[]{:S(2)}, u32[]{:S(2)}) collective-permute-start(bf16[192,7168]{1,0:T(8,128)(2,1)} %bitcast.4), channel_id=1, source_target_pairs={{0,8},{8,16},{16,24},{24,0},{1,9},{9,17},{17,25},{25,1},{2,10},{10... | collective-permute-start | bytes 8257544 | tf_op jit(solution)/shard_map/ppermute | solution.py:57
  79.3 73.8 %collective-permute-start.2 = (bf16[192,7168]{1,0:T(8,128)(2,1)}, bf16[192,7168]{1,0:T(8,128)(2,1)}, u32[]{:S(2)}, u32[]{:S(2)}) collective-permute-start(bf16[192,7168]{1,0:T(8,128)(2,1)} %bitcast.4), channel_id=1, source_target_pairs={{0,24},{8,0},{16,8},{24,16},{1,25},{9,1},{17,9},{25,17},{2,26},{10... | collective-permute-start | bytes 8257544 | tf_op jit(solution)/shard_map/ppermute | solution.py:62
  140.0 61.0 %collective-permute-start.3 = (bf16[192,7168]{1,0:T(8,128)(2,1)}, bf16[192,7168]{1,0:T(8,128)(2,1)}, u32[]{:S(2)}, u32[]{:S(2)}) collective-permute-start(bf16[192,7168]{1,0:T(8,128)(2,1)} %collective-permute-done.1), channel_id=1, source_target_pairs={{0,8},{8,16},{16,24},{24,0},{1,9},{9,17},{17,25},{25,1},{2,10},{10... | collective-permute-start | bytes 8257544 | tf_op jit(solution)/shard_map/ppermute | solution.py:57
  150.8 52.3 %slice-start = ((s8[7340032]{0:T(1024)(128)(4,1)}), s8[4194304]{0:T(1024)(128)(4,1)S(1)}, s32[]{:S(2)}) async-start(s8[7340032]{0:T(1024)(128)(4,1)} %bitcast.35), calls=%async_computation.4 | async-start | bytes 8388608
  153.0 50.1 %slice-start.1 = ((s8[7340032]{0:T(1024)(128)(4,1)}), s8[3145728]{0:T(1024)(128)(4,1)S(1)}, s32[]{:S(2)}) async-start(s8[7340032]{0:T(1024)(128)(4,1)} %bitcast.35), calls=%async_computation.5 | async-start | bytes 6291456
  203.1 7.0 %copy-start = (bf16[1,1,256,7168]{3,2,1,0:T(8,128)(2,1)S(1)}, bf16[1,1,256,7168]{3,2,1,0:T(8,128)(2,1)}, u32[]{:S(2)}) copy-start(bf16[1,1,256,7168]{3,2,1,0:T(8,128)(2,1)} %param.9) | copy-start | bytes 11010052
  319.5 5.2 %copy-start.1 = (f32[1,64,2]{1,2,0:T(2,128)S(1)}, f32[1,64,2]{1,2,0:T(2,128)}, u32[]{:S(2)}) copy-start(f32[1,64,2]{1,2,0:T(2,128)} %param.7) | copy-start | bytes 1540
  319.5 38.5 %all-to-all-start.1 = ((bf16[8,24,7168]{2,1,0:T(8,128)(2,1)}), bf16[8,24,7168]{2,1,0:T(8,128)(2,1)}, u32[]{:S(2)}, u32[]{:S(2)}) async-start(bf16[8,24,7168]{2,1,0:T(8,128)(2,1)} %bitcast.38), calls=%async_computation.2 | async-start | bytes 5505024 | tf_op jit(solution)/shard_map/all_to_all | solution.py:75
Sparse Core Ops, SparseCore 0:
  217.5 101.9 reduce-scatter.1
